TPU v7x, 32 devices: a whole 2x2x4 slice. The times are simulated.
32 devices in a mesh: row: 4 (over y, core), col: 8 (over z, x).
Axes of the slice: x: 2, y: 2, z: 4, core: 2. Of those that a mesh axis runs over, the one named last changes fastest.
Arguments:
- singles: bfloat16 [96, 384], P(('row', 'col')), may hold values from -6 to 6
- pair: float32 [96, 96, 128], P('row', 'col'), may hold values from -48 to 48
- frames: float32 [96, 12], P(('row', 'col')), may hold values from -9 to 9, as said below
- w_query: bfloat16 [384, 336], replicated, may hold values from -0.3125 to 0.3125
- w_keyval: bfloat16 [384, 816], replicated, may hold values from -0.3125 to 0.3125
- w_bias: float32 [128, 12], replicated, may hold values from -1 to 1
- head_weights: float32 [12], replicated, may hold values from -2 to 1
- w_out: bfloat16 [2112, 384], replicated, may hold values from -0.125 to 0.125
Outputs:
- update: float32 [96, 384], P(('row', 'col'))
Inputs may be any that keep to these rules, and one draw needn't show every extreme that they name: `frames`: the first nine entries of a row are a rotation matrix in row-major order, the last three a translation.
All inputs are finite; a program needn't handle non-finite values.
Results may differ from a plain program's by a relative error of at most 0.0029.
Values sent between devices are 32-bit elements; how exact they have to be, the bound alone decides.
A program may use at most 64 MiB of HBM per device.

v0:
```python
import math

import jax
import jax.numpy as jnp
from jax import lax
from jax.sharding import PartitionSpec as P

CS = 384
CZ = 128
H = 12
CH = 16
PQ = 4
PV = 8


HIGHEST = lax.Precision.HIGHEST


def broadcast(value, axis, source):
    kept = jnp.where(lax.axis_index(axis) == source, value, 0).astype(value.dtype)
    return lax.psum(kept, axis)


def rigid_apply(frames, points):
    rotation = frames[:, :9].reshape(frames.shape[0], 3, 3)
    moved = jnp.einsum("nab,nbm->nam", rotation, points, precision=HIGHEST)
    return moved + frames[:, 9:12, None]


def query_side(singles, frames, w_query):
    row_count = singles.shape[0]
    scalar_width = H * CH
    projected = jnp.dot(singles, w_query, preferred_element_type=jnp.float32)
    points = rigid_apply(frames, projected[:, scalar_width:].reshape(row_count, 3, H * PQ))
    return jnp.concatenate([projected[:, :scalar_width], points.reshape(row_count, 3 * H * PQ)], 1)


def key_side(singles, frames, w_keyval):
    row_count = singles.shape[0]
    scalar_width = 2 * H * CH
    point_end = scalar_width + 3 * H * PQ
    projected = jnp.dot(singles, w_keyval, preferred_element_type=jnp.float32)
    key_points = rigid_apply(
        frames, projected[:, scalar_width:point_end].reshape(row_count, 3, H * PQ)
    )
    value_points = rigid_apply(frames, projected[:, point_end:].reshape(row_count, 3, H * PV))
    return jnp.concatenate(
        [
            projected[:, :scalar_width],
            key_points.reshape(row_count, 3 * H * PQ),
            value_points.reshape(row_count, 3 * H * PV),
        ],
        1,
    )


def logits_of(query_feat, key_feat, pair_block, w_bias, head_weights):
    query_rows = query_feat.shape[0]
    key_rows = key_feat.shape[0]
    scalar_width = H * CH
    query_vec = query_feat[:, :scalar_width].reshape(query_rows, H, CH)
    query_points = query_feat[:, scalar_width:].reshape(query_rows, 3, H, PQ)
    key_vec = key_feat[:, :scalar_width].reshape(key_rows, H, CH)
    key_points = key_feat[:, 2 * scalar_width : 2 * scalar_width + 3 * H * PQ].reshape(
        key_rows, 3, H, PQ
    )
    scalar = jnp.einsum("ihc,jhc->ihj", query_vec, key_vec, precision=HIGHEST) / math.sqrt(CH)
    pair_bias = jnp.einsum("ijc,ch->ihj", pair_block, w_bias, precision=HIGHEST)
    cross_term = jnp.einsum("iahp,jahp->ihj", query_points, key_points, precision=HIGHEST)
    query_square = jnp.sum(query_points * query_points, axis=(1, 3))
    key_square = jnp.sum(key_points * key_points, axis=(1, 3))
    distance = query_square[:, :, None] + key_square.T[None, :, :] - 2.0 * cross_term
    weight = jax.nn.softplus(head_weights) * (math.sqrt(2.0 / (9.0 * PQ)) / 2.0)
    return math.sqrt(1.0 / 3.0) * (scalar + pair_bias - weight[None, :, None] * distance)


def weighted(exponent, key_feat, pair_block):
    key_rows = key_feat.shape[0]
    scalar_width = H * CH
    value_vec = key_feat[:, scalar_width : 2 * scalar_width].reshape(key_rows, H, CH)
    value_points = key_feat[:, 2 * scalar_width + 3 * H * PQ :].reshape(key_rows, 3, H, PV)
    weight_sum = jnp.sum(exponent, axis=2)
    scalar = jnp.einsum("ihj,jhc->ihc", exponent, value_vec, precision=HIGHEST)
    points = jnp.einsum("ihj,jahp->iahp", exponent, value_points, precision=HIGHEST)
    paired = jnp.einsum("ihj,ijc->ihc", exponent, pair_block, precision=HIGHEST)
    return (weight_sum, scalar, points, paired)


def finish_rest(scalar, points, frames, w_out):
    row_count = scalar.shape[0]
    rotation = frames[:, :9].reshape(row_count, 3, 3)
    relative = points - frames[:, 9:12, None, None]
    local_points = jnp.einsum("nba,nbhp->nahp", rotation, relative, precision=HIGHEST)
    length = jnp.sqrt(jnp.sum(local_points * local_points, axis=1) + 1.0)
    features = jnp.concatenate(
        [
            scalar.reshape(row_count, H * CH),
            local_points.reshape(row_count, 3 * H * PV),
            length.reshape(row_count, H * PV),
        ],
        1,
    )
    features = features.astype(jnp.bfloat16)
    return jnp.dot(features, w_out[: H * (CH + 4 * PV)], preferred_element_type=jnp.float32)


def paired_term(paired, w_out):
    row_count = paired.shape[0]
    pair_rows = w_out[H * (CH + 4 * PV) :].astype(jnp.float32)
    return jnp.dot(paired.reshape(row_count, H * CZ), pair_rows, precision=HIGHEST)


def finish(weight_sum, scalar, points, paired, frames, w_out):
    scalar = scalar / weight_sum[:, :, None]
    points = points / weight_sum[:, None, :, None]
    paired = paired / weight_sum[:, :, None]
    return finish_rest(scalar, points, frames, w_out) + paired_term(paired, w_out)


def block_size(total):
    chosen_size = 1
    for candidate in range(1, min(total, 32) + 1):
        if total % candidate == 0:
            chosen_size = candidate
    return chosen_size


def by_blocks(compute, arrays, total):
    size = block_size(total)
    count = total // size

    def one_block(start):
        pieces = [lax.dynamic_slice_in_dim(array, start, size, 0) for array in arrays]
        return compute(*pieces)

    starts = jnp.arange(count) * size
    results = lax.map(one_block, starts)
    return jax.tree.map(lambda value: value.reshape((total,) + value.shape[2:]), results)


def blocked_logits(query_feat, key_feat, pair, w_bias, head_weights):

    def compute(query_part, pair_part):
        return logits_of(query_part, key_feat, pair_part, w_bias, head_weights)

    return by_blocks(compute, [query_feat, pair], pair.shape[0])


def blocked_weighted(logits, shift, key_feat, pair):

    def compute(logit_part, shift_part, pair_part):
        return weighted(jnp.exp(logit_part - shift_part[:, :, None]), key_feat, pair_part)

    return by_blocks(compute, [logits, shift, pair], pair.shape[0])


def body(singles, pair, frames, w_query, w_keyval, w_bias, head_weights, w_out):
    rows_dev = singles.shape[0]
    query_rows = pair.shape[0]
    key_rows = pair.shape[1]
    column = lax.axis_index("col")
    ratio = query_rows // key_rows
    source = column // ratio
    within = column % ratio * key_rows
    packed = jnp.concatenate([singles.astype(jnp.float32), frames], 1)
    row_packed = lax.all_gather(packed, "col", axis=0, tiled=True)
    chosen = lax.dynamic_slice_in_dim(row_packed, within, key_rows, 0)
    arrived = broadcast(chosen, "row", source)
    query_feat = query_side(row_packed[:, :CS].astype(jnp.bfloat16), row_packed[:, CS:], w_query)
    key_feat = key_side(arrived[:, :CS].astype(jnp.bfloat16), arrived[:, CS:], w_keyval)
    logits = blocked_logits(query_feat, key_feat, pair, w_bias, head_weights)
    local_peak = jnp.max(logits, axis=2)
    own_start = column * rows_dev
    peak = lax.pmax(local_peak, "col")
    part_sum, part_scalar, part_points, part_paired = blocked_weighted(logits, peak, key_feat, pair)
    summed = lax.psum((part_sum, part_scalar, part_points, part_paired), "col")
    weight_sum, scalar, points, paired = [
        lax.dynamic_slice_in_dim(piece, own_start, rows_dev, 0) for piece in summed
    ]
    return finish(weight_sum, scalar, points, paired, frames, w_out)


def solution(mesh):
    return jax.shard_map(
        body,
        mesh=mesh,
        in_specs=(
            P(("row", "col"), None),
            P("row", "col", None),
            P(("row", "col"), None),
            P(),
            P(),
            P(),
            P(),
            P(),
        ),
        out_specs=P(("row", "col"), None),
        check_vma=False,
    )
```

profile of v0, /device:TPU:0, one launch (start us, length us, event | category | flops | bytes accessed | tf_op | source)
XLA Modules:
  0.0 156.1 jit_solution(14814837688478335846)
XLA Ops:
  6.6 0.7 convert_element_type.4
  7.3 0.7 maximum_bitcast_fusion
  8.0 32.3 %all-gather = f32[8,3,396]{2,1,0:T(4,128)S(1)} all-gather(f32[1,3,396]{2,1,0:T(4,128)S(1)} %maximum_bitcast_fusion), channel_id=1, replica_groups=mesh['row'=4,'col'=8] {'col'}, dimensions={0}, use_global_device_ids=true | all-gather | bytes 42768 | tf_op jit(solution)/shard_map/all_gather | solution.py:166
  40.5 10.3 %psum.35 = f32[12,396]{1,0:T(8,128)S(1)} all-reduce(f32[12,396]{1,0:T(8,128)S(1)} %dynamic-slice_select_fusion), channel_id=1, replica_groups=mesh['row'=4,'col'=8] {'row'}, use_global_device_ids=true, to_apply=%region_0.1 | all-reduce | flops 4752 | bytes 38016 | tf_op jit(solution)/shard_map/psum | solution.py:21
  50.9 1.1 fusion.22
  52.1 0.3 fusion.23
  52.6 0.2 multiply_reduce_fusion.2
  52.9 0.1 copy.56
  53.2 0.3 multiply_reduce_fusion.1
  53.9 0.1 copy.47
  54.1 0.8 fusion.24
  54.9 0.4 fusion.9
  55.3 0.3 fusion.37
  55.6 21.6 %pmax.7 = f32[24,12]{0,1:T(8,128)S(1)} all-reduce(f32[24,12]{0,1:T(8,128)S(1)} %get-tuple-element.60), channel_id=1, replica_groups=mesh['row'=4,'col'=8] {'col'}, use_global_device_ids=true, to_apply=%region_6.7 | all-reduce | flops 288 | bytes 2304 | tf_op jit(solution)/shard_map/pmax | solution.py:174
  77.2 0.2 copy.68
  77.4 1.0 fusion.15
  78.6 0.2 convolution_add_fusion.1
  78.9 0.1 copy.60
  79.0 0.4 convolution_bitcast_fusion
  79.4 0.1 copy.73
  79.5 0.2 convolution_bitcast_fusion.1
  79.8 36.4 %all-reduce = (f32[24,3,12,8]{0,3,1,2:T(8,128)S(1)}, f32[24,12]{0,1:T(8,128)S(1)}, f32[24,12,16]{0,2,1:T(8,128)S(1)}) all-reduce(f32[24,3,12,8]{0,3,1,2:T(8,128)S(1)} %convolution_bitcast_fusion, f32[24,12]{0,1:T(8,128)S(1)} %get-tuple-element.40, ...), channel_id=1, replica_groups=mesh['row'=4,'col'=8] {'col'}, use_global_device_ids=true, to_apply=%region_10.11 | all-reduce | flops 11808 | bytes 94464 | tf_op jit(solution)/shard_map/psum | solution.py:176
  116.4 0.1 divide_subtract_fusion
  116.5 0.3 copy.63
  116.9 0.3 convert_bitcast_fusion
  117.3 0.1 sqrt.8
  117.4 0.1 copy.65
  117.6 0.1 reshape.86
  117.9 0.2 fusion.13
  118.1 29.1 %all-reduce.3.cloned.1.call-done = f32[24,12,128]{2,1,0:T(8,128)} async-done(((f32[24,12,128]{2,1,0:T(8,128)}), f32[24,12,128]{2,1,0:T(8,128)}) %all-reduce.3.cloned.1.call-update) | async-done | bytes 147472 | tf_op jit(solution)/shard_map/psum | solution.py:176
  147.2 0.8 divide_bitcast_fusion
  148.1 1.2 fusion.10
  (47 shorter events, 2.1 us)
Async XLA Ops:
  6.5 45.6 %copy-start = (bf16[384,816]{0,1:T(8,128)(2,1)S(1)}, bf16[384,816]{0,1:T(8,128)(2,1)}, u32[]{:S(2)}) copy-start(bf16[384,816]{0,1:T(8,128)(2,1)} %param.12) | copy-start | bytes 1880068
  6.5 47.3 %copy-start.5 = (f32[12]{0:T(128)S(1)}, f32[12]{0:T(128)}, u32[]{:S(2)}) copy-start(f32[12]{0:T(128)} %param.14) | copy-start | bytes 148
  6.5 47.5 %copy-start.2 = (f32[24,12,128]{2,0,1:T(8,128)S(1)}, f32[24,12,128]{2,0,1:T(8,128)}, u32[]{:S(2)}) copy-start(f32[24,12,128]{2,0,1:T(8,128)} %param.9) | copy-start | bytes 442372
  6.5 47.5 %copy-start.4 = (f32[128,12]{0,1:T(8,128)S(1)}, f32[128,12]{0,1:T(8,128)}, u32[]{:S(2)}) copy-start(f32[128,12]{0,1:T(8,128)} %param.13) | copy-start | bytes 18436
  6.5 140.7 %all-reduce.3.cloned.1.call-start = ((), (), s32[]{:S(2)}) async-start(), calls=%async_computation | async-start | bytes 393216 | tf_op jit(solution)/shard_map/psum | solution.py:176
  53.0 25.5 %copy-start.3 = (f32[3,12]{1,0:T(4,128)S(1)}, f32[3,12]{1,0:T(4,128)}, u32[]{:S(2)}) copy-start(f32[3,12]{1,0:T(4,128)} %param.10) | copy-start | bytes 436
  77.4 40.5 %copy-start.1 = (bf16[2112,384]{1,0:T(8,128)(2,1)S(1)}, bf16[2112,384]{1,0:T(8,128)(2,1)}, u32[]{:S(2)}) copy-start(bf16[2112,384]{1,0:T(8,128)(2,1)} %param.15) | copy-start | bytes 4866052
Sparse Core Ops, SparseCore 0:
  78.5 68.6 all-reduce.2
where the time goes:
time: 156 us
  blocking collectives  101 us (65%)
  waiting for transfers between devices  29.1 us (19%)
  between operations  13.7 us (9%)
  matrix products  6.99 us (4%)
  local copies, waits for them, and re-layouts  3.08 us (2%)
  other arithmetic  2.58 us (2%)
    psum x1, blocking collectives, body(): summed = lax.psum((part_sum, part_scalar, part_points, part_paired), 'col')  36.4 us
    all_gather x1, blocking collectives, body(): row_packed = lax.all_gather(packed, 'col', axis=0, tiled=True)  32.3 us
    psum x1, waiting for transfers between devices, body(): summed = lax.psum((part_sum, part_scalar, part_points, part_paired), 'col')  29.1 us
    pmax x1, blocking collectives, body(): peak = lax.pmax(local_peak, 'col')  21.6 us
    psum x1, blocking collectives, broadcast(): return lax.psum(kept, axis)  10.3 us
  transfers between devices with their start and end apart: 1, of which 1 were waited for; matrix products, arithmetic and copies ran while one was open for 2% of the time, Pallas kernels for 0%

commit v1 on v0

v1 whole, which is shorter than its diff:
```python
import functools
import math

import jax
import jax.numpy as jnp
from jax import lax
from jax.experimental import pallas as pl
from jax.experimental.pallas import tpu as pltpu
from jax.sharding import PartitionSpec as P

CS = 384
CZ = 128
H = 12
CH = 16
PQ = 4
PV = 8

HP = 16
LANES = 128
HIGHEST = lax.Precision.HIGHEST
MESH = pl.DeviceIdType.MESH
NT = (((1,), (1,)), ((), ()))
NN = (((1,), (0,)), ((), ()))


def round_up(value, step):
    return (value + step - 1) // step * step


def dot_exact(left, right, dims):
    return lax.dot_general(
        left, right, dims, precision=HIGHEST, preferred_element_type=jnp.float32
    )


def head_mask(width, offset, per_head, heads_period):
    feature = lax.broadcasted_iota(jnp.int32, (HP, width), 1) - offset
    head = lax.broadcasted_iota(jnp.int32, (HP, width), 0)
    return (feature % heads_period) // per_head == head


def moved_points(frame, local, width):
    parts = [local[:, b * width : (b + 1) * width] for b in range(3)]
    return [
        frame[:, 3 * a : 3 * a + 1] * parts[0]
        + frame[:, 3 * a + 1 : 3 * a + 2] * parts[1]
        + frame[:, 3 * a + 2 : 3 * a + 3] * parts[2]
        + frame[:, 9 + a : 10 + a]
        for a in range(3)
    ]


def kernel(
    sizes,
    singles_ref,
    frames_ref,
    w_bias_ref,
    heads_ref,
    pair_hbm,
    w_query_hbm,
    w_keyval_hbm,
    w_out_hbm,
    out_ref,
    x_all,
    pair_own,
    pair_all,
    w_query_ref,
    w_keyval_ref,
    w_out_ref,
    k_feat,
    v_feat,
    load_sem,
    x_send,
    x_recv,
    p_send,
    p_recv,
):
    row_devs, col_devs = sizes
    devices = row_devs * col_devs
    rows = singles_ref.shape[0]
    keys = pair_own.shape[1]
    key_pad = round_up(keys, 8)
    slots = col_devs * key_pad
    row = lax.axis_index("row")
    col = lax.axis_index("col")
    me = row * col_devs + col
    own_rows = pl.ds(col * rows, rows)

    loads = [
        pltpu.make_async_copy(pair_hbm, pair_own, load_sem.at[0]),
        pltpu.make_async_copy(pair_hbm.at[own_rows], pair_all.at[:, col], load_sem.at[1]),
        pltpu.make_async_copy(w_query_hbm, w_query_ref, load_sem.at[2]),
        pltpu.make_async_copy(w_keyval_hbm, w_keyval_ref, load_sem.at[3]),
        pltpu.make_async_copy(w_out_hbm, w_out_ref, load_sem.at[4]),
    ]
    for load in loads:
        load.start()

    barrier = pltpu.get_barrier_semaphore()

    def greet(step, carry):
        peer = lax.rem(me + step, devices)
        pl.semaphore_signal(
            barrier,
            inc=1,
            device_id=(peer // col_devs, lax.rem(peer, col_devs)),
            device_id_type=MESH,
        )
        return carry

    lax.fori_loop(1, devices, greet, 0)

    def slot_of(device):
        first = device * rows
        return first // keys * key_pad + lax.rem(first, keys)

    for c in range(col_devs):
        for slot in range(c * key_pad + keys, (c + 1) * key_pad):
            x_all[slot] = jnp.zeros(x_all.shape[1:], jnp.float32)
    single = singles_ref[...]
    frame = frames_ref[...]
    own_slot = pl.ds(slot_of(me), rows)
    for t in range(CS // LANES):
        x_all[own_slot, t, :] = single[:, t * LANES : (t + 1) * LANES].astype(jnp.float32)
    x_all[own_slot, CS // LANES, :] = jnp.concatenate(
        [frame, jnp.zeros((rows, LANES - 12), jnp.float32)], 1
    )
    loads[0].wait()
    pl.semaphore_wait(barrier, devices - 1)

    def x_copy(slot_device, peer, send_index, recv_index):
        slot = pl.ds(slot_of(slot_device), rows)
        return pltpu.make_async_remote_copy(
            src_ref=x_all.at[slot],
            dst_ref=x_all.at[slot],
            send_sem=x_send.at[send_index],
            recv_sem=x_recv.at[recv_index],
            device_id=(peer // col_devs, lax.rem(peer, col_devs)),
            device_id_type=MESH,
        )

    def p_copy(peer_col, sent_col, send_index, recv_index):
        return pltpu.make_async_remote_copy(
            src_ref=pair_own.at[pl.ds(peer_col * rows, rows)],
            dst_ref=pair_all.at[:, sent_col],
            send_sem=p_send.at[send_index],
            recv_sem=p_recv.at[recv_index],
            device_id=(row, peer_col),
            device_id_type=MESH,
        )

    def send_x(step, carry):
        x_copy(me, lax.rem(me + step, devices), step, me).start()
        return carry

    def send_p(step, carry):
        p_copy(lax.rem(col + step, col_devs), col, step, col).start()
        return carry

    lax.fori_loop(1, devices, send_x, 0)
    lax.fori_loop(1, col_devs, send_p, 0)

    scalar = H * CH
    loads[2].wait()
    projected = jnp.dot(single, w_query_ref[...], preferred_element_type=jnp.float32)
    q_points = moved_points(frame, projected[:, scalar:], H * PQ)
    q_feat = jnp.concatenate([projected[:, :scalar]] + q_points, 1)

    raw = heads_ref[...]
    gamma_row = jnp.maximum(raw, 0.0) + jnp.log(1.0 + jnp.exp(-jnp.abs(raw)))
    eye = lax.broadcasted_iota(jnp.int32, (HP, H), 0) == lax.broadcasted_iota(
        jnp.int32, (HP, H), 1
    )
    gamma = jnp.sum(jnp.where(eye, gamma_row, 0.0), axis=1, keepdims=True)
    weight = gamma * (math.sqrt(2.0 / (9.0 * PQ)) / 2.0)
    scalar_part = jnp.where(head_mask(scalar, 0, CH, scalar), 1.0 / math.sqrt(CH), 0.0)
    point_mask = head_mask(3 * H * PQ, 0, PQ, H * PQ)
    point_part = jnp.where(point_mask, 2.0 * weight, 0.0)
    square_part = jnp.where(point_mask, -weight, 0.0)
    q_scale = jnp.concatenate([scalar_part, point_part], 1)
    spread = jnp.concatenate(
        [
            jnp.concatenate([q_feat[i : i + 1] * q_scale, square_part], 1)
            for i in range(rows)
        ],
        0,
    )
    q_square = [
        jnp.sum(
            jnp.where(point_mask, q_feat[i : i + 1, scalar:] ** 2, 0.0), axis=1, keepdims=True
        )
        * weight
        for i in range(rows)
    ]
    bias_weights = w_bias_ref[...]

    def wait_x(step, carry):
        source = lax.rem(me + devices - step, devices)
        x_copy(source, source, step, source).wait_recv()
        return carry

    lax.fori_loop(1, devices, wait_x, 0)
    loads[3].wait()

    chunk = LANES if slots % LANES == 0 else slots

    def key_side(start):
        part = pl.ds(start, chunk)
        inputs = [x_all[part, t, :].astype(jnp.bfloat16) for t in range(CS // LANES)]
        held = x_all[part, CS // LANES, :]
        values = jnp.dot(
            jnp.concatenate(inputs, 1), w_keyval_ref[...], preferred_element_type=jnp.float32
        )
        key_end = 2 * scalar + 3 * H * PQ
        key_points = moved_points(held, values[:, 2 * scalar : key_end], H * PQ)
        value_points = moved_points(held, values[:, key_end:], H * PV)
        squares = [point * point for point in key_points]
        k_feat[part, :] = jnp.concatenate([values[:, :scalar]] + key_points + squares, 1)
        v_feat[part, :] = jnp.concatenate([values[:, scalar : 2 * scalar]] + value_points, 1)

    if chunk == slots:
        key_side(0)
    else:

        @pl.loop(0, slots // chunk)
        def _(index):
            key_side(pl.multiple_of(index * chunk, chunk))

    inner = dot_exact(spread, k_feat[...], NT)

    def wait_p(step, carry):
        source = lax.rem(col + col_devs - step, col_devs)
        p_copy(source, source, step, source).wait_recv()
        return carry

    loads[1].wait()
    lax.fori_loop(1, col_devs, wait_p, 0)

    place = lax.rem(lax.broadcasted_iota(jnp.int32, (HP, slots), 1), key_pad)
    bias_rows = jnp.concatenate([bias_weights, jnp.zeros((CZ, HP - H), jnp.float32)], 1).T
    shares, pooled = [], []
    for i in range(rows):
        block = pair_all[i]
        if key_pad != keys:
            block = jnp.concatenate(
                [block, jnp.zeros((col_devs, key_pad - keys, CZ), jnp.float32)], 1
            )
        block = block.reshape(slots, CZ)
        bias = dot_exact(bias_rows, block, NT)
        logits = math.sqrt(1.0 / 3.0) * (inner[i * HP : (i + 1) * HP] + bias - q_square[i])
        if key_pad != keys:
            logits = jnp.where(place < keys, logits, -jnp.inf)
        exponent = jnp.exp(logits - jnp.max(logits, axis=1, keepdims=True))
        share = exponent / jnp.sum(exponent, axis=1, keepdims=True)
        shares.append(share)
        pooled.append(dot_exact(share, block, NN))

    gathered = dot_exact(jnp.concatenate(shares, 0), v_feat[...], NN)
    value_masks = [head_mask(scalar, 0, CH, scalar), head_mask(3 * H * PV, 0, PV, H * PV)]
    value_mask = jnp.concatenate([jnp.where(mask, 1.0, 0.0) for mask in value_masks], 1)
    kept = jnp.concatenate(
        [
            jnp.sum(
                gathered[i * HP : (i + 1) * HP] * value_mask,
                axis=0,
                keepdims=True,
            )
            for i in range(rows)
        ],
        0,
    )
    wide = H * PV
    relative = [
        kept[:, scalar + b * wide : scalar + (b + 1) * wide] - frame[:, 9 + b : 10 + b]
        for b in range(3)
    ]
    local = [
        frame[:, a : a + 1] * relative[0]
        + frame[:, 3 + a : 4 + a] * relative[1]
        + frame[:, 6 + a : 7 + a] * relative[2]
        for a in range(3)
    ]
    length = jnp.sqrt(local[0] ** 2 + local[1] ** 2 + local[2] ** 2 + 1.0)
    loads[4].wait()
    features = jnp.concatenate([kept[:, :scalar]] + local + [length], 1).astype(jnp.bfloat16)
    split = H * (CH + 4 * PV)
    total = jnp.dot(features, w_out_ref[0:split, :], preferred_element_type=jnp.float32)
    flat = jnp.concatenate(
        [
            jnp.concatenate([pooled[i][h : h + 1] for i in range(rows)], 0)
            for h in range(H)
        ],
        1,
    )
    high = flat.astype(jnp.bfloat16)
    rest = flat - high.astype(jnp.float32)
    middle = rest.astype(jnp.bfloat16)
    low = (rest - middle.astype(jnp.float32)).astype(jnp.bfloat16)
    w_pair = w_out_ref[split:, :]
    for piece in (low, middle, high):
        total = total + jnp.dot(piece, w_pair, preferred_element_type=jnp.float32)
    out_ref[...] = total

    def end_x(step, carry):
        peer = lax.rem(me + step, devices)
        x_copy(me, peer, step, me).wait_send()
        return carry

    def end_p(step, carry):
        p_copy(lax.rem(col + step, col_devs), col, step, col).wait_send()
        return carry

    lax.fori_loop(1, devices, end_x, 0)
    lax.fori_loop(1, col_devs, end_p, 0)


def solution(mesh):
    sizes = (mesh.shape["row"], mesh.shape["col"])
    devices = sizes[0] * sizes[1]

    def body(singles, pair, frames, w_query, w_keyval, w_bias, head_weights, w_out):
        rows = singles.shape[0]
        keys = pair.shape[1]
        slots = sizes[1] * round_up(keys, 8)
        vmem = pl.BlockSpec(memory_space=pltpu.VMEM)
        hbm = pl.BlockSpec(memory_space=pl.ANY)
        return pl.pallas_call(
            functools.partial(kernel, sizes),
            out_shape=jax.ShapeDtypeStruct((rows, w_out.shape[1]), jnp.float32),
            in_specs=[vmem] * 4 + [hbm] * 4,
            out_specs=vmem,
            scratch_shapes=[
                pltpu.VMEM((slots, CS // LANES + 1, LANES), jnp.float32),
                pltpu.VMEM(pair.shape, jnp.float32),
                pltpu.VMEM((rows, sizes[1], keys, CZ), jnp.float32),
                pltpu.VMEM(w_query.shape, w_query.dtype),
                pltpu.VMEM(w_keyval.shape, w_keyval.dtype),
                pltpu.VMEM(w_out.shape, w_out.dtype),
                pltpu.VMEM((slots, H * CH + 6 * H * PQ), jnp.float32),
                pltpu.VMEM((slots, H * CH + 3 * H * PV), jnp.float32),
                pltpu.SemaphoreType.DMA((5,)),
                pltpu.SemaphoreType.DMA((devices,)),
                pltpu.SemaphoreType.DMA((devices,)),
                pltpu.SemaphoreType.DMA((sizes[1],)),
                pltpu.SemaphoreType.DMA((sizes[1],)),
            ],
            compiler_params=pltpu.CompilerParams(
                collective_id=0, has_side_effects=True, vmem_limit_bytes=60 * 2**20
            ),
        )(
            singles,
            frames,
            w_bias,
            head_weights.reshape(1, H),
            pair,
            w_query,
            w_keyval,
            w_out,
        )

    return jax.shard_map(
        body,
        mesh=mesh,
        in_specs=(
            P(("row", "col"), None),
            P("row", "col", None),
            P(("row", "col"), None),
            P(),
            P(),
            P(),
            P(),
            P(),
        ),
        out_specs=P(("row", "col"), None),
        check_vma=False,
    )
```

time: 156 us -> 30.9 us (0.20)
  blocking collectives: 101 us -> 0 us
  waiting for transfers between devices: 29.1 us -> 0 us
  Pallas kernels: 0 us -> 22.2 us
  between operations: 13.7 us -> 0.01 us
  matrix products: 6.99 us -> 0 us
  local copies, waits for them, and re-layouts: 3.08 us -> 8.35 us
  other arithmetic: 2.58 us -> 0 us
    psum x2 -> x0, blocking collectives: 46.6 us -> none  [the longest x1 36.4 us: body(): summed = lax.psum((part_sum, part_scalar, part_points, part_paired), 'col')]
    all_gather x1 -> x0, blocking collectives: 32.3 us -> none  [body(): row_packed = lax.all_gather(packed, 'col', axis=0, tiled=True)]
    psum x1 -> x0, waiting for transfers between devices: 29.1 us -> none  [body(): summed = lax.psum((part_sum, part_scalar, part_points, part_paired), 'col')]
    pallas_call x0 -> x1, Pallas kernels: none -> 22.2 us  [body(): pl.pallas_call(functools.partial(kernel, sizes), out_shape=jax.ShapeDtype...]
    pmax x1 -> x0, blocking collectives: 21.6 us -> none  [body(): peak = lax.pmax(local_peak, 'col')]
    unnamed x13 -> x5, local copies, waits for them, and re-layouts: 0.05 us -> 8.35 us
    dot_general x14 -> x0, matrix products: 6.99 us -> none  [the longest x1 1.17 us: paired_term(): jnp.dot(paired.reshape(row_count, H * CZ), pair_rows, precision=HIGHEST)]
  transfers between devices with their start and end apart: 1 -> 0, of which waited for: 1 -> 0; matrix products, arithmetic and copies ran while one was open for 2% -> 0% of each run, Pallas kernels for 0% -> 0%
where the time goes in v1:
time: 30.9 us; the launch traced here: 30.6 us
  Pallas kernels  22.2 us (72%)
  local copies, waits for them, and re-layouts  8.35 us (27%)
    pallas_call x1, Pallas kernels, body(): pl.pallas_call(functools.partial(kernel, sizes), out_shape=jax.ShapeDtype...  22.2 us
    unnamed x5, local copies, waits for them, and re-layouts  8.35 us

profile of v1, /device:TPU:0, one launch (start us, length us, event | category | flops | bytes accessed | tf_op | source)
XLA Modules:
  0.0 30.6 jit_solution(17767886756264637650)
XLA Ops:
  0.0 1.4 %copy.9.w_bias_ref = f32[128,12]{1,0:T(8,128)} copy(f32[128,12]{0,1:T(8,128)} %param.13) | data formatting | bytes 12288 | tf_op args[5]
  1.4 1.6 %copy.10.pair_hbm = f32[24,12,128]{2,1,0:T(8,128)} copy(f32[24,12,128]{2,0,1:T(8,128)} %param.9) | data formatting | bytes 294912 | tf_op args[1]
  3.0 1.8 %copy.11.w_query_hbm = bf16[384,336]{1,0:T(8,128)(2,1)} copy(bf16[384,336]{0,1:T(8,128)(2,1)} %param.11) | data formatting | bytes 516096 | tf_op args[3]
  4.9 2.2 %copy.12.w_keyval_hbm = bf16[384,816]{1,0:T(8,128)(2,1)} copy(bf16[384,816]{0,1:T(8,128)(2,1)} %param.12) | data formatting | bytes 1253376 | tf_op args[4]
  7.1 22.2 %shard_map.82 = f32[3,384]{1,0:T(4,128)} custom-call(bf16[3,384]{1,0:T(4,128)(2,1)} %singles_ref.1, f32[3,12]{1,0:T(4,128)} %frames_ref.1, f32[128,12]{1,0:T(8,128)} %copy.9.w_bias_ref, f32[1,12]{1,0:T(1,128)} %bitcast.1, f32[24,12,128]{2,1,0:T(8,128)} %copy.10.pair_hbm, bf16[384,336]{1,0:T(8,128)(2,1)} %copy.11.w_query_hbm, ...), custom_call_target="tpu_custom_call" | custom-call | tf_op jit(solution)/shard_map/pallas_call | solution.py:327
  29.3 1.3 %copy.14 = f32[3,384]{1,0:T(4,128)} copy(f32[3,384]{1,0:T(4,128)} %shard_map.82) | data formatting | bytes 9216

commit v2 on v1

--- a/solution.py
+++ b/solution.py
@@ -46,6 +46,17 @@
         + frame[:, 3 * a + 1 : 3 * a + 2] * parts[1]
         + frame[:, 3 * a + 2 : 3 * a + 3] * parts[2]
         + frame[:, 9 + a : 10 + a]
+        for a in range(3)
+    ]
+
+
+def moved_columns(frame, local, width):
+    parts = [local[b * width : (b + 1) * width] for b in range(3)]
+    return [
+        frame[3 * a : 3 * a + 1] * parts[0]
+        + frame[3 * a + 1 : 3 * a + 2] * parts[1]
+        + frame[3 * a + 2 : 3 * a + 3] * parts[2]
+        + frame[9 + a : 10 + a]
         for a in range(3)
     ]
 
@@ -62,6 +73,7 @@
     w_out_hbm,
     out_ref,
     x_all,
+    pair_raw,
     pair_own,
     pair_all,
     w_query_ref,
@@ -84,14 +96,12 @@
     row = lax.axis_index("row")
     col = lax.axis_index("col")
     me = row * col_devs + col
-    own_rows = pl.ds(col * rows, rows)
 
     loads = [
-        pltpu.make_async_copy(pair_hbm, pair_own, load_sem.at[0]),
-        pltpu.make_async_copy(pair_hbm.at[own_rows], pair_all.at[:, col], load_sem.at[1]),
-        pltpu.make_async_copy(w_query_hbm, w_query_ref, load_sem.at[2]),
-        pltpu.make_async_copy(w_keyval_hbm, w_keyval_ref, load_sem.at[3]),
-        pltpu.make_async_copy(w_out_hbm, w_out_ref, load_sem.at[4]),
+        pltpu.make_async_copy(pair_hbm, pair_raw, load_sem.at[0]),
+        pltpu.make_async_copy(w_query_hbm, w_query_ref, load_sem.at[1]),
+        pltpu.make_async_copy(w_keyval_hbm, w_keyval_ref, load_sem.at[2]),
+        pltpu.make_async_copy(w_out_hbm, w_out_ref, load_sem.at[3]),
     ]
     for load in loads:
         load.start()
@@ -126,6 +136,10 @@
         [frame, jnp.zeros((rows, LANES - 12), jnp.float32)], 1
     )
     loads[0].wait()
+    for i in range(pair_own.shape[0]):
+        pair_own[i] = pair_raw[:, i, :]
+    for i in range(rows):
+        pair_all[i, col] = pair_own[col * rows + i]
     pl.semaphore_wait(barrier, devices - 1)
 
     def x_copy(slot_device, peer, send_index, recv_index):
@@ -161,8 +175,10 @@
     lax.fori_loop(1, col_devs, send_p, 0)
 
     scalar = H * CH
-    loads[2].wait()
-    projected = jnp.dot(single, w_query_ref[...], preferred_element_type=jnp.float32)
+    loads[1].wait()
+    projected = lax.dot_general(
+        single, w_query_ref[...], NT, preferred_element_type=jnp.float32
+    )
     q_points = moved_points(frame, projected[:, scalar:], H * PQ)
     q_feat = jnp.concatenate([projected[:, :scalar]] + q_points, 1)
 
@@ -200,23 +216,26 @@
         return carry
 
     lax.fori_loop(1, devices, wait_x, 0)
-    loads[3].wait()
+    loads[2].wait()
 
     chunk = LANES if slots % LANES == 0 else slots
 
     def key_side(start):
         part = pl.ds(start, chunk)
         inputs = [x_all[part, t, :].astype(jnp.bfloat16) for t in range(CS // LANES)]
-        held = x_all[part, CS // LANES, :]
-        values = jnp.dot(
-            jnp.concatenate(inputs, 1), w_keyval_ref[...], preferred_element_type=jnp.float32
-        )
-        key_end = 2 * scalar + 3 * H * PQ
-        key_points = moved_points(held, values[:, 2 * scalar : key_end], H * PQ)
-        value_points = moved_points(held, values[:, key_end:], H * PV)
+        held = x_all[part, CS // LANES, :].T
+        values = lax.dot_general(
+            w_keyval_ref[...],
+            jnp.concatenate(inputs, 1),
+            NT,
+            preferred_element_type=jnp.float32,
+        )
+        first, second = 2 * scalar, 2 * scalar + 3 * H * PQ
+        key_points = moved_columns(held, values[first:second], H * PQ)
+        value_points = moved_columns(held, values[second:], H * PV)
         squares = [point * point for point in key_points]
-        k_feat[part, :] = jnp.concatenate([values[:, :scalar]] + key_points + squares, 1)
-        v_feat[part, :] = jnp.concatenate([values[:, scalar : 2 * scalar]] + value_points, 1)
+        k_feat[:, part] = jnp.concatenate([values[:scalar]] + key_points + squares, 0)
+        v_feat[:, part] = jnp.concatenate([values[scalar:first]] + value_points, 0)
 
     if chunk == slots:
         key_side(0)
@@ -226,18 +245,17 @@
         def _(index):
             key_side(pl.multiple_of(index * chunk, chunk))
 
-    inner = dot_exact(spread, k_feat[...], NT)
+    inner = dot_exact(spread, k_feat[...], NN)
 
     def wait_p(step, carry):
         source = lax.rem(col + col_devs - step, col_devs)
         p_copy(source, source, step, source).wait_recv()
         return carry
 
-    loads[1].wait()
     lax.fori_loop(1, col_devs, wait_p, 0)
 
     place = lax.rem(lax.broadcasted_iota(jnp.int32, (HP, slots), 1), key_pad)
-    bias_rows = jnp.concatenate([bias_weights, jnp.zeros((CZ, HP - H), jnp.float32)], 1).T
+    bias_rows = jnp.concatenate([bias_weights, jnp.zeros((HP - H, CZ), jnp.float32)], 0)
     shares, pooled = [], []
     for i in range(rows):
         block = pair_all[i]
@@ -255,7 +273,7 @@
         shares.append(share)
         pooled.append(dot_exact(share, block, NN))
 
-    gathered = dot_exact(jnp.concatenate(shares, 0), v_feat[...], NN)
+    gathered = dot_exact(jnp.concatenate(shares, 0), v_feat[...], NT)
     value_masks = [head_mask(scalar, 0, CH, scalar), head_mask(3 * H * PV, 0, PV, H * PV)]
     value_mask = jnp.concatenate([jnp.where(mask, 1.0, 0.0) for mask in value_masks], 1)
     kept = jnp.concatenate(
@@ -281,7 +299,7 @@
         for a in range(3)
     ]
     length = jnp.sqrt(local[0] ** 2 + local[1] ** 2 + local[2] ** 2 + 1.0)
-    loads[4].wait()
+    loads[3].wait()
     features = jnp.concatenate([kept[:, :scalar]] + local + [length], 1).astype(jnp.bfloat16)
     split = H * (CH + 4 * PV)
     total = jnp.dot(features, w_out_ref[0:split, :], preferred_element_type=jnp.float32)
@@ -331,14 +349,15 @@
             out_specs=vmem,
             scratch_shapes=[
                 pltpu.VMEM((slots, CS // LANES + 1, LANES), jnp.float32),
+                pltpu.VMEM((keys, pair.shape[0], CZ), jnp.float32),
                 pltpu.VMEM(pair.shape, jnp.float32),
                 pltpu.VMEM((rows, sizes[1], keys, CZ), jnp.float32),
-                pltpu.VMEM(w_query.shape, w_query.dtype),
-                pltpu.VMEM(w_keyval.shape, w_keyval.dtype),
+                pltpu.VMEM(w_query.shape[::-1], w_query.dtype),
+                pltpu.VMEM(w_keyval.shape[::-1], w_keyval.dtype),
                 pltpu.VMEM(w_out.shape, w_out.dtype),
-                pltpu.VMEM((slots, H * CH + 6 * H * PQ), jnp.float32),
-                pltpu.VMEM((slots, H * CH + 3 * H * PV), jnp.float32),
-                pltpu.SemaphoreType.DMA((5,)),
+                pltpu.VMEM((H * CH + 6 * H * PQ, slots), jnp.float32),
+                pltpu.VMEM((H * CH + 3 * H * PV, slots), jnp.float32),
+                pltpu.SemaphoreType.DMA((4,)),
                 pltpu.SemaphoreType.DMA((devices,)),
                 pltpu.SemaphoreType.DMA((devices,)),
                 pltpu.SemaphoreType.DMA((sizes[1],)),
@@ -350,11 +369,11 @@
         )(
             singles,
             frames,
-            w_bias,
+            w_bias.T,
             head_weights.reshape(1, H),
-            pair,
-            w_query,
-            w_keyval,
+            pair.transpose(1, 0, 2),
+            w_query.T,
+            w_keyval.T,
             w_out,
         )
 

time: 30.9 us -> 21.7 us (0.70)
  local copies, waits for them, and re-layouts: 8.35 us -> 1.29 us
  Pallas kernels: 22.2 us -> 20.2 us
    unnamed x5 -> x1, local copies, waits for them, and re-layouts: 8.35 us -> 1.29 us
    pallas_call x1, Pallas kernels: 22.2 us -> 20.2 us  [body(): pl.pallas_call(functools.partial(kernel, sizes), out_shape=jax.ShapeDtype...]
where the time goes in v2:
time: 21.7 us; the launch traced here: 21.5 us
  Pallas kernels  20.2 us (93%)
  local copies, waits for them, and re-layouts  1.29 us (6%)
    pallas_call x1, Pallas kernels, body(): pl.pallas_call(functools.partial(kernel, sizes), out_shape=jax.ShapeDtype...  20.2 us
    unnamed x1, local copies, waits for them, and re-layouts  1.29 us

profile of v2, /device:TPU:0, one launch (start us, length us, event | category | flops | bytes accessed | tf_op | source)
XLA Modules:
  0.0 21.5 jit_solution(8511480224721152386)
XLA Ops:
  0.0 20.2 %shard_map.82 = f32[3,384]{1,0:T(4,128)} custom-call(bf16[3,384]{1,0:T(4,128)(2,1)} %singles_ref.1, f32[3,12]{1,0:T(4,128)} %frames_ref.1, f32[12,128]{1,0:T(8,128)} %bitcast.8, f32[1,12]{1,0:T(1,128)} %bitcast.9, f32[12,24,128]{2,1,0:T(8,128)} %bitcast.7, bf16[336,384]{1,0:T(8,128)(2,1)} %bitcast.6, bf16[816,384]{1,0:T(8,128)(2,1)} %bitcast.5, ...), custom_call_target="tpu_custom_call" | custom-call | tf_op jit(solution)/shard_map/pallas_call | solution.py:345
  20.2 1.3 %copy.10 = f32[3,384]{1,0:T(4,128)} copy(f32[3,384]{1,0:T(4,128)} %shard_map.82) | data formatting | bytes 9216

commit v3 on v2

--- a/solution.py
+++ b/solution.py
@@ -107,18 +107,31 @@
         load.start()
 
     barrier = pltpu.get_barrier_semaphore()
+    core = lax.rem(row, 2)
+    place_in_plane = row // 2 * col_devs + col
+    plane = devices // 2
+
+    def in_plane(step):
+        index = lax.rem(place_in_plane + step, plane)
+        return (index // col_devs * 2 + core, lax.rem(index, col_devs))
+
+    def partner_of(peer):
+        return (peer[0] // 2 * 2 + 1 - lax.rem(peer[0], 2), peer[1])
+
+    def number_of(peer):
+        return peer[0] * col_devs + peer[1]
+
+    here = (row, col)
+
+    def greet_one(peer):
+        pl.semaphore_signal(barrier, inc=1, device_id=peer, device_id_type=MESH)
 
     def greet(step, carry):
-        peer = lax.rem(me + step, devices)
-        pl.semaphore_signal(
-            barrier,
-            inc=1,
-            device_id=(peer // col_devs, lax.rem(peer, col_devs)),
-            device_id_type=MESH,
-        )
-        return carry
-
-    lax.fori_loop(1, devices, greet, 0)
+        greet_one(in_plane(step))
+        return carry
+
+    lax.fori_loop(1, plane, greet, 0)
+    greet_one(partner_of(here))
 
     def slot_of(device):
         first = device * rows
@@ -140,18 +153,26 @@
         pair_own[i] = pair_raw[:, i, :]
     for i in range(rows):
         pair_all[i, col] = pair_own[col * rows + i]
-    pl.semaphore_wait(barrier, devices - 1)
-
-    def x_copy(slot_device, peer, send_index, recv_index):
-        slot = pl.ds(slot_of(slot_device), rows)
+    pl.semaphore_wait(barrier, plane)
+
+    def x_copy(source, peer, send_index):
+        number = number_of(source)
+        slot = pl.ds(slot_of(number), rows)
         return pltpu.make_async_remote_copy(
             src_ref=x_all.at[slot],
             dst_ref=x_all.at[slot],
             send_sem=x_send.at[send_index],
-            recv_sem=x_recv.at[recv_index],
-            device_id=(peer // col_devs, lax.rem(peer, col_devs)),
+            recv_sem=x_recv.at[number],
+            device_id=peer,
             device_id_type=MESH,
         )
+
+    def x_direct(step):
+        peer = in_plane(step)
+        return x_copy(here, peer, number_of(peer))
+
+    def x_relay(source):
+        return x_copy(source, partner_of(here), number_of(partner_of(source)))
 
     def p_copy(peer_col, sent_col, send_index, recv_index):
         return pltpu.make_async_remote_copy(
@@ -164,14 +185,15 @@
         )
 
     def send_x(step, carry):
-        x_copy(me, lax.rem(me + step, devices), step, me).start()
+        x_direct(step).start()
         return carry
 
     def send_p(step, carry):
         p_copy(lax.rem(col + step, col_devs), col, step, col).start()
         return carry
 
-    lax.fori_loop(1, devices, send_x, 0)
+    lax.fori_loop(1, plane, send_x, 0)
+    x_relay(here).start()
     lax.fori_loop(1, col_devs, send_p, 0)
 
     scalar = H * CH
@@ -210,12 +232,18 @@
     ]
     bias_weights = w_bias_ref[...]
 
+    def pass_on(step, carry):
+        source = in_plane(plane - step)
+        x_relay(source).wait_recv()
+        x_relay(source).start()
+        return carry
+
     def wait_x(step, carry):
-        source = lax.rem(me + devices - step, devices)
-        x_copy(source, source, step, source).wait_recv()
-        return carry
-
-    lax.fori_loop(1, devices, wait_x, 0)
+        x_relay(partner_of(in_plane(plane - step))).wait_recv()
+        return carry
+
+    lax.fori_loop(1, plane, pass_on, 0)
+    lax.fori_loop(0, plane, wait_x, 0)
     loads[2].wait()
 
     chunk = LANES if slots % LANES == 0 else slots
@@ -320,15 +348,16 @@
     out_ref[...] = total
 
     def end_x(step, carry):
-        peer = lax.rem(me + step, devices)
-        x_copy(me, peer, step, me).wait_send()
+        x_direct(step).wait_send()
+        x_relay(in_plane(step)).wait_send()
         return carry
 
     def end_p(step, carry):
         p_copy(lax.rem(col + step, col_devs), col, step, col).wait_send()
         return carry
 
-    lax.fori_loop(1, devices, end_x, 0)
+    x_relay(here).wait_send()
+    lax.fori_loop(1, plane, end_x, 0)
     lax.fori_loop(1, col_devs, end_p, 0)
 
 

time: 21.7 us -> 19 us (0.88)
  the two profiles are of different devices: /device:TPU:0 before, /device:TPU:3 now
where the time goes in v3:
time: 19 us; the launch traced here: 18.8 us
  Pallas kernels  17.5 us (92%)
  local copies, waits for them, and re-layouts  1.29 us (7%)
    pallas_call x1, Pallas kernels, body(): pl.pallas_call(functools.partial(kernel, sizes), out_shape=jax.ShapeDtype...  17.5 us
    unnamed x1, local copies, waits for them, and re-layouts  1.29 us

profile of v3, /device:TPU:3, one launch (start us, length us, event | category | flops | bytes accessed | tf_op | source)
XLA Modules:
  0.0 18.8 jit_solution(2687193923748161707)
XLA Ops:
  0.0 17.5 %shard_map.82 = f32[3,384]{1,0:T(4,128)} custom-call(bf16[3,384]{1,0:T(4,128)(2,1)} %singles_ref.1, f32[3,12]{1,0:T(4,128)} %frames_ref.1, f32[12,128]{1,0:T(8,128)} %bitcast.8, f32[1,12]{1,0:T(1,128)} %bitcast.9, f32[12,24,128]{2,1,0:T(8,128)} %bitcast.7, bf16[336,384]{1,0:T(8,128)(2,1)} %bitcast.6, bf16[816,384]{1,0:T(8,128)(2,1)} %bitcast.5, ...), custom_call_target="tpu_custom_call" | custom-call | tf_op jit(solution)/shard_map/pallas_call | solution.py:374
  17.5 1.3 %copy.10 = f32[3,384]{1,0:T(4,128)} copy(f32[3,384]{1,0:T(4,128)} %shard_map.82) | data formatting | bytes 9216
